TPU v7x, 32 devices: a whole 2x2x4 slice. The times are simulated.
32 devices in a mesh: row: 4 (over y, core), col: 8 (over z, x).
Axes of the slice: x: 2, y: 2, z: 4, core: 2. Of those that a mesh axis runs over, the one named last changes fastest.
Arguments:
- covariance: float32 [16384, 16384], P('row', 'col'), as said below
- weights: float32 [16384], P(('row', 'col')), may hold values from 0.5 to 1
- dual_slacks: float32 [16384], P(('row', 'col')), may hold values from 2.5 to 10
- returns: float32 [16384], P(('row', 'col')), may hold values from -6 to 6
- targets: float32 [256], P('col'), may hold values from 0.5 to 1
- sector_duals: float32 [256], replicated, may hold values from -6 to 6
- lengths: int32 [256], replicated, may hold values from 1 to 1024, 16384 in all
Outputs:
- factored: float32 [16384, 16384], P('row', 'col')
- solved_rhs: float32 [16384], P('row')
- sector_cols: float32 [16384, 256], P('row', 'col')
- sector_resid: float32 [256], P('col')
Inputs may be any that keep to these rules, and one draw needn't show every extreme that they name: `lengths`: lengths sum to 16384. `covariance`: only the lower triangle with the diagonal is read; with the added diagonal the system is positive definite.
All inputs are finite; a program needn't handle non-finite values.
Results may differ from a plain program's by a relative error of at most 0.0003.
Values sent between devices are 32-bit elements; how exact they have to be, the bound alone decides.
A program may use at most 192 MiB of HBM per device.

v0:
```python
import jax
import jax.numpy as jnp
from jax import lax
from jax.experimental import pallas as pl
from jax.experimental.pallas import tpu as pltpu
from jax.sharding import PartitionSpec as P

NB = 128
PANELS = 8


HIGHEST = lax.Precision.HIGHEST
HIGH = lax.Precision.HIGH
SIGMA_GAP = 0.5
NT = (((1,), (1,)), ((), ()))


def eliminate(block):
    width = block.shape[0]
    rows = lax.broadcasted_iota(jnp.int32, (width, width), 0)
    lanes = lax.broadcasted_iota(jnp.int32, (width, width), 1)

    def step(j, carry):
        left, right = carry
        at_row = rows == j
        row = jnp.sum(jnp.where(at_row, left, 0.0), axis=0, keepdims=True)
        other = jnp.sum(jnp.where(at_row, right, 0.0), axis=0, keepdims=True)
        column = jnp.sum(jnp.where(lanes == j, left, 0.0), axis=1, keepdims=True)
        pivot = jnp.sum(jnp.where(lanes[:1] == j, row, 0.0), axis=1, keepdims=True)
        scale = lax.rsqrt(pivot)
        scale = scale * (1.5 - 0.5 * pivot * scale * scale)
        row = row * scale
        other = other * scale
        column = column * scale
        below = rows > j
        left = jnp.where(below, left - column * row, jnp.where(at_row, row, left))
        right = jnp.where(below, right - column * other, jnp.where(at_row, other, right))
        return (left, right)

    identity = (rows == lanes).astype(jnp.float32)
    upper, inverse = lax.fori_loop(0, width, step, (block, identity))
    upper = jnp.where(lanes >= rows, upper, 0.0)
    return (upper.T, inverse)


def factor_kernel(head_ref, factor_ref, inverse_ref):
    order = head_ref.shape[0]
    factor_ref[...] = head_ref[...]
    inverse_ref[...] = jnp.zeros_like(inverse_ref)
    for first in range(0, order, NB):
        last = first + NB
        here = slice(first, last)
        lower, inverse = eliminate(factor_ref[here, here])
        factor_ref[here, here] = lower
        inverse_ref[here, here] = inverse
        if first:
            done = jnp.dot(
                factor_ref[here, :first],
                inverse_ref[:first, :first],
                precision=HIGHEST,
                preferred_element_type=jnp.float32,
            )
            inverse_ref[here, :first] = -jnp.dot(
                inverse, done, precision=HIGHEST, preferred_element_type=jnp.float32
            )
        if last < order:
            below = lax.dot_general(
                factor_ref[last:, here], inverse, NT, precision=HIGHEST,
                preferred_element_type=jnp.float32,
            )
            factor_ref[last:, here] = below
            factor_ref[here, last:] = jnp.zeros((NB, order - last), jnp.float32)
            for top in range(last, order, NB):
                factor_ref[top:, top:top + NB] -= lax.dot_general(
                    below[top - last:], below[top - last:top - last + NB], NT,
                    precision=HIGHEST, preferred_element_type=jnp.float32,
                )


def lower_inverse(symmetric):
    order = symmetric.shape[0]
    shape = jax.ShapeDtypeStruct((order, order), jnp.float32)
    return pl.pallas_call(
        factor_kernel,
        out_shape=(shape, shape),
        in_specs=[pl.BlockSpec(memory_space=pltpu.VMEM)],
        out_specs=(pl.BlockSpec(memory_space=pltpu.VMEM),) * 2,
        compiler_params=pltpu.CompilerParams(vmem_limit_bytes=48 * 1024 * 1024),
        cost_estimate=pl.CostEstimate(
            flops=200 * order**3, bytes_accessed=12 * order * order, transcendentals=order
        ),
    )(symmetric)


def on_device(covariance, weights, dual_slacks, returns, targets, sector_duals, lengths):
    tile_rows, tile_cols = covariance.shape
    row_devices, col_devices = lax.axis_size("row"), lax.axis_size("col")
    order_total = tile_rows * row_devices
    row_id = lax.axis_index("row")
    col_id = lax.axis_index("col")
    row_start = row_id * tile_rows
    col_start = col_id * tile_cols
    sectors_here = targets.shape[0]
    lead = PANELS * NB
    piece = tile_rows // col_devices

    head_raw = jnp.where((row_id == 0) & (col_id == 0), covariance[:lead, :lead], 0.0)
    head_raw = lax.psum(head_raw, ("row", "col"))
    lead_raw = jnp.where(col_id == 0, covariance[:, :lead], 0.0)
    lead_raw = lax.psum_scatter(lead_raw, "col", scatter_dimension=0, tiled=True)

    stacked = jnp.stack([weights, dual_slacks, returns])
    full = lax.all_gather(stacked, ("row", "col"), axis=1, tiled=True)
    full_weights, full_slacks, full_returns = full[0], full[1], full[2]
    full_diag = full_slacks / full_weights

    head = jnp.tril(head_raw)
    symmetric = head + jnp.tril(head_raw, -1).T
    eye = jnp.arange(lead)[:, None] == jnp.arange(lead)[None, :]
    symmetric = symmetric + jnp.where(eye, full_diag[:lead, None], 0.0)
    factor, inverse = lower_inverse(symmetric)

    mine = lax.dot_general(lead_raw, inverse, NT, precision=HIGH)
    piece_id = row_id * col_devices + col_id
    piece_start = piece_id * piece
    padded = jnp.pad(factor, ((0, max(0, piece - lead % piece) if lead % piece else 0), (0, 0)))
    head_rows = lax.dynamic_slice_in_dim(
        padded, jnp.minimum(piece_start, padded.shape[0] - piece), piece
    )
    piece_index = piece_start + jnp.arange(piece, dtype=jnp.int32)
    mine = jnp.where((piece_index < lead)[:, None], head_rows, mine)
    count = row_devices * col_devices
    moves = []
    for source in range(count):
        target_row, target_col = source % row_devices, source // row_devices
        moves.append((source, target_row * col_devices + target_col))
    moved = lax.ppermute(mine, ("row", "col"), moves)
    cols_factor = lax.all_gather(moved, "row", axis=0, tiled=True)
    rows_factor = lax.all_gather(mine, "col", axis=0, tiled=True)

    sector_ends = jnp.cumsum(lengths)
    offsets = sector_ends - lengths
    mean_gap = jnp.sum(full_weights * full_slacks) / order_total
    sector_first = col_id * sectors_here
    local_offsets = lax.dynamic_slice_in_dim(offsets, sector_first, sectors_here)
    local_ends = lax.dynamic_slice_in_dim(sector_ends, sector_first, sectors_here)
    sector_sizes = lax.dynamic_slice_in_dim(lengths, sector_first, sectors_here).astype(jnp.float32)
    all_assets = jnp.arange(order_total, dtype=jnp.int32)
    column_member = (all_assets[None, :] >= local_offsets[:, None]) & (
        all_assets[None, :] < local_ends[:, None]
    )
    held = jnp.sum(jnp.where(column_member, full_weights[None, :], 0.0), axis=1)
    sector_resid = targets - held / sector_sizes

    global_rows = row_start + jnp.arange(tile_rows, dtype=jnp.int32)
    global_cols = col_start + jnp.arange(tile_cols, dtype=jnp.int32)
    lower_mask = global_rows[:, None] >= global_cols[None, :]
    strict_mask = global_rows[:, None] > global_cols[None, :]
    weight_rows = lax.dynamic_slice_in_dim(full_weights, row_start, tile_rows)
    weight_cols = lax.dynamic_slice_in_dim(full_weights, col_start, tile_cols)
    row_part = jnp.sum(jnp.where(lower_mask, covariance * weight_cols[None, :], 0.0), axis=1)
    col_part = jnp.sum(jnp.where(strict_mask, covariance * weight_rows[:, None], 0.0), axis=0)
    zeros = jnp.zeros((order_total,), jnp.float32)
    partial_value = lax.dynamic_update_slice_in_dim(
        zeros, row_part, row_start, 0
    ) + lax.dynamic_update_slice_in_dim(zeros, col_part, col_start, 0)
    partial_value, symmetric = lax.optimization_barrier((partial_value, symmetric))
    product = lax.psum(partial_value, ("row", "col"))

    def right_sides(start, size):
        index = start + jnp.arange(size, dtype=jnp.int32)
        cut = lambda value: lax.dynamic_slice_in_dim(value, start, size)
        member = (index[:, None] >= offsets[None, :]) & (index[:, None] < sector_ends[None, :])
        prices = jnp.sum(jnp.where(member, sector_duals[None, :], 0.0), axis=1)
        rhs = cut(full_returns) - cut(product) - prices + SIGMA_GAP * mean_gap / cut(full_weights)
        local = (index[:, None] >= local_offsets[None, :]) & (index[:, None] < local_ends[None, :])
        columns = local.astype(jnp.float32) * lax.rsqrt(sector_sizes)[None, :]
        return jnp.concatenate([rhs[:, None], columns], axis=1)

    solved_head = jnp.dot(inverse, right_sides(0, lead), precision=HIGHEST)
    extras = right_sides(row_start, tile_rows)

    update = lax.dot_general(rows_factor, cols_factor, NT, precision=HIGH)
    diag_rows = lax.dynamic_slice_in_dim(full_diag, row_start, tile_rows)
    on_diagonal = global_rows[:, None] == global_cols[None, :]
    work = covariance - update + jnp.where(on_diagonal, diag_rows[:, None], 0.0)
    lead_part = jnp.pad(rows_factor, ((0, 0), (0, tile_cols - lead)))
    work = jnp.where((global_cols < lead)[None, :], lead_part, work)
    factored = jnp.where(lower_mask, work, 0.0)

    extras = extras - jnp.dot(rows_factor, solved_head, precision=HIGHEST)
    top = jnp.where(row_id == 0, solved_head, extras[:lead])
    extras = lax.dynamic_update_slice_in_dim(extras, top, 0, 0)
    return (factored, extras[:, 0], extras[:, 1:], sector_resid)


def solution(mesh):
    return jax.shard_map(
        on_device,
        mesh=mesh,
        in_specs=(
            P("row", "col"),
            P(("row", "col")),
            P(("row", "col")),
            P(("row", "col")),
            P("col"),
            P(),
            P(),
        ),
        out_specs=(P("row", "col"), P("row"), P("row", "col"), P("col")),
        check_vma=False,
    )
```

profile of v0, /device:TPU:29, one launch (start us, length us, event | category | flops | bytes accessed | tf_op | source)
XLA Modules:
  0.0 1012.4 jit_solution(1934086697790889304)
XLA Ops:
  8.1 4.8 slice.38
  12.8 5.4 copy.32
  18.2 2.8 broadcast_select_fusion
  21.1 12.5 %slice_select_fusion = f32[4096,1024]{1,0:T(8,128)} fusion(f32[4096,2048]{1,0:T(8,128)} %param.7, pred[]{:T(512)S(6)} %eq.13), kind=kLoop, calls=%fused_computation.4 | loop fusion | flops 4194304 | bytes 33554432 | tf_op jit(solution)/shard_map/jit(_where)/select_n | solution.py:109
  34.3 68.2 %all_gather.9 = f32[3,16384]{1,0:T(4,128)S(1)} all-gather(f32[3,512]{1,0:T(4,128)S(1)} %pad_maximum_fusion), channel_id=1, replica_groups=mesh['row'=4,'col'=8] {'row','col'}, dimensions={1}, use_global_device_ids=true | all-gather | bytes 202752 | tf_op jit(solution)/shard_map/all_gather | solution.py:113
  105.3 16.4 %select_reduce_fusion = (f32[2048]{0:T(1024)S(1)}, f32[4096]{0:T(1024)S(1)}) fusion(f32[4096,2048]{1,0:T(8,128)} %param.7, f32[4096]{0:T(1024)S(1)} %bitcast.29, s32[2048]{0:T(1024)S(1)} %iota_add_fusion.1, s32[4096]{0:T(1024)S(1)} %iota_add_fusion, f32[2048]{0:T(1024)S(1)} %bitcast.33), kind=kLoop, calls=%fused_computation.3 | loop fusion | flops 67102720 | bytes 33628160 | tf_op jit(solution)/shard_map/reduce_sum | solution.py:162
  122.4 1.4 dynamic_update_slice.11
  124.3 1.3 add_dynamic-update-slice_fusion
  125.6 173.8 %all-reduce.4.cloned.1.call-done = f32[1024,1024]{0,1:T(8,128)} async-done(((f32[1024,1024]{0,1:T(8,128)}), f32[1024,1024]{0,1:T(8,128)}) %all-reduce.4.cloned.1.call-update) | async-done | bytes 4194320 | tf_op jit(solution)/shard_map/psum | solution.py:108
  299.4 5.5 copy.30
  305.0 6.1 bitcast_add_fusion
  311.0 5.4 copy.31
  316.4 4.8 select_add_fusion.head_ref
  321.3 165.4 %shard_map.102 = (f32[1024,1024]{1,0:T(8,128)S(1)}, f32[1024,1024]{1,0:T(8,128)}) custom-call(f32[1024,1024]{1,0:T(8,128)} %select_add_fusion.head_ref), custom_call_target="tpu_custom_call" | custom-call | flops 214748364800 | bytes 12582912 | tf_op jit(solution)/shard_map/pallas_call | solution.py:83
  486.7 1.9 copy-done
  488.7 8.3 dynamic-slice_select_fusion
  497.2 9.1 collective-permute-start
  506.3 154.4 %collective-permute-done = f32[512,1024]{1,0:T(8,128)S(1)} collective-permute-done((f32[512,1024]{1,0:T(8,128)}, f32[512,1024]{1,0:T(8,128)S(1)}, u32[]{:S(2)}, u32[]{:S(2)}) %collective-permute-start) | collective-permute-done | bytes 2097184 | tf_op jit(solution)/shard_map/ppermute | solution.py:137
  660.7 1.3 copy-done.1
  666.7 1.3 select_reduce_fusion.1
  668.9 239.5 %all-reduce.6.cloned.1.call-done = f32[16384]{0:T(1024)} async-done(((f32[16384]{0:T(1024)}), f32[16384]{0:T(1024)}) %all-reduce.6.cloned.1.call-update) | async-done | bytes 65552 | tf_op jit(solution)/shard_map/psum | solution.py:168
  909.9 6.2 fusion.4
  916.1 19.4 %convolution_subtract_fusion = f32[4096,33]{0,1:T(8,128)S(1)} fusion(f32[4096,1024]{1,0:T(8,128)} %all-gather.3.cloned.1.call-done, f32[1024,33]{0,1:T(8,128)S(1)} %fusion.4, f32[4096,32]{0,1:T(8,128)S(1)} %and_select_fusion, f32[4096,1]{0,1:T(1,128)S(1)} %bitcast.31), kind=kOutput, calls=%fused_computation.5 | convolution fusion | flops 1661214720 | bytes 17993728 | tf_op jit(solution)/shard_map/dot_general | solution.py:191
  937.0 67.4 %compare_select_fusion.1 = f32[4096,2048]{1,0:T(8,128)} fusion(f32[4096,2048]{1,0:T(8,128)} %param.7, f32[4096,1024]{1,0:T(8,128)} %all-gather.3.cloned.1.call-done, f32[2048,1024]{1,0:T(8,128)} %all-gather.5.cloned.1.call-done, f32[4096]{0:T(1024)S(1)} %dynamic_slice.42, s32[2048]{0:T(1024)S(1)} %copy-done.11, s32[4096]{0:T(1024)S(1)} %copy-done.6, ...), kind=kOutput, calls=%fused_computation.1 | convolution fusion | flops 51598327808 | bytes 92317696 | tf_op jit(solution)/shard_map/dot_general | solution.py:183
  (81 shorter events, 12.6 us)
Async XLA Ops:
  8.0 291.4 %all-reduce.4.cloned.1.call-start = ((), (), s32[]{:S(2)}) async-start(), calls=%async_computation.1 | async-start | bytes 8388608 | tf_op jit(solution)/shard_map/psum | solution.py:108
  21.1 467.7 %reduce-scatter.2.cloned.1.call-start = ((), (), s32[]{:S(2)}) async-start(), calls=%async_computation.2 | async-start | bytes 18874368 | tf_op jit(solution)/shard_map/reduce_scatter | solution.py:110
  33.6 0.7 copy-start.14
  33.6 0.7 copy-start.15
  33.6 0.7 copy-start.16
  33.6 874.8 %all-reduce.6.cloned.1.call-start = ((), (), s32[]{:S(2)}) async-start(), calls=%async_computation.5 | async-start | bytes 131072 | tf_op jit(solution)/shard_map/psum | solution.py:168
  102.5 0.7 copy-start.2
  104.0 17.8 %copy-start.3 = (f32[1,16384]{1,0:T(1,128)}, f32[1,16384]{1,0:T(1,128)S(1)}, u32[]{:S(2)}) copy-start(f32[1,16384]{1,0:T(1,128)S(1)} %get-tuple-element.15) | copy-start | bytes 196612
  105.3 16.5 %copy-start.10 = (s32[2048]{0:T(1024)}, s32[2048]{0:T(1024)S(1)}, u32[]{:S(2)}) copy-start(s32[2048]{0:T(1024)S(1)} %iota_add_fusion.1) | copy-start | bytes 24580
  105.3 16.5 %copy-start.5 = (s32[4096]{0:T(1024)}, s32[4096]{0:T(1024)S(1)}, u32[]{:S(2)}) copy-start(s32[4096]{0:T(1024)S(1)} %iota_add_fusion) | copy-start | bytes 49156
  105.3 16.5 %copy-start.7 = (f32[1,4096]{1,0:T(1,128)}, f32[1,4096]{1,0:T(1,128)S(1)}, u32[]{:S(2)}) copy-start(f32[1,4096]{1,0:T(1,128)S(1)} %constant_dynamic-slice_fusion) | copy-start | bytes 49156
  321.3 167.5 %copy-start.17 = (pred[512]{0:T(512)(128)(4,1)S(1)}, pred[512]{0:T(512)(128)(4,1)}, u32[]{:S(2)}) copy-start(pred[512]{0:T(512)(128)(4,1)} %add_compare_fusion) | copy-start | bytes 1540
  486.7 1.9 copy-start
  488.7 427.4 %all-gather.3.cloned.1.call-start = ((), (), s32[]{:S(2)}) async-start(), calls=%async_computation.3 | async-start | bytes 18874368 | tf_op jit(solution)/shard_map/all_gather | solution.py:139
  497.1 165.7 %copy-start.12 = (s32[256]{0:T(256)S(1)}, s32[256]{0:T(256)}, u32[]{:S(2)}) copy-start(s32[256]{0:T(256)} %param.13) | copy-start | bytes 3076
  497.1 167.2 %copy-start.13 = (f32[256]{0:T(256)S(1)}, f32[256]{0:T(256)}, u32[]{:S(2)}) copy-start(f32[256]{0:T(256)} %param.12) | copy-start | bytes 3076
  497.1 167.4 %copy-start.4 = (f32[1,16384]{1,0:T(1,128)S(1)}, f32[1,16384]{1,0:T(1,128)}, u32[]{:S(2)}) copy-start(f32[1,16384]{1,0:T(1,128)} %copy-done.3) | copy-start | bytes 196612
  497.1 168.1 %copy-start.18 = (f32[32]{0:T(128)S(1)}, f32[32]{0:T(128)}, u32[]{:S(2)}) copy-start(f32[32]{0:T(128)} %param.11) | copy-start | bytes 388
  497.1 169.6 %copy-start.6 = (s32[4096]{0:T(1024)S(1)}, s32[4096]{0:T(1024)}, u32[]{:S(2)}) copy-start(s32[4096]{0:T(1024)} %copy-done.5) | copy-start | bytes 49156
  497.1 412.0 %copy-start.8 = (f32[1,4096]{1,0:T(1,128)S(1)}, f32[1,4096]{1,0:T(1,128)}, u32[]{:S(2)}) copy-start(f32[1,4096]{1,0:T(1,128)} %copy-done.7) | copy-start | bytes 49156
  497.1 439.9 %all-gather.5.cloned.1.call-start = ((), (), s32[]{:S(2)}) async-start(), calls=%async_computation.4 | async-start | bytes 10485760 | tf_op jit(solution)/shard_map/all_gather | solution.py:138
  497.2 163.5 %collective-permute-start = (f32[512,1024]{1,0:T(8,128)}, f32[512,1024]{1,0:T(8,128)S(1)}, u32[]{:S(2)}, u32[]{:S(2)}) collective-permute-start(f32[512,1024]{1,0:T(8,128)} %dynamic-slice_select_fusion), channel_id=1, source_target_pairs={{0,0},{1,8},{2,16},{3,24},{4,1},{5,9},{6,17},{7,25},{8,2},{9,10},{... | collective-permute-start | bytes 6291464 | tf_op jit(solution)/shard_map/ppermute | solution.py:137
  660.7 1.3 copy-start.1
  916.1 20.9 %copy-start.11 = (s32[2048]{0:T(1024)S(1)}, s32[2048]{0:T(1024)}, u32[]{:S(2)}) copy-start(s32[2048]{0:T(1024)} %copy-done.10) | copy-start | bytes 24580
  (1 other events, 0.6 us)
Sparse Core Ops, SparseCore 0:
  21.2 278.2 all-reduce.3
  488.8 419.6 all-reduce.5
Sparse Core Ops, SparseCore 1:
  33.7 301.7 reduce-scatter.1
  497.2 305.5 all-gather.2
  804.2 57.5 all-gather.4
where the time goes:
time: 1030 us; the launch traced here: 1010 us
  waiting for transfers between devices  568 us (55%)
  Pallas kernels  165 us (16%)
  matrix products  101 us (10%)
  blocking collectives  68.2 us (7%)
  other arithmetic  50.8 us (5%)
  local copies, waits for them, and re-layouts  32.5 us (3%)
  between operations  17 us (2%)
    psum x1, waiting for transfers between devices, on_device(): product = lax.psum(partial_value, ('row', 'col'))  240 us
    psum x1, waiting for transfers between devices, on_device(): head_raw = lax.psum(head_raw, ('row', 'col'))  174 us
    pallas_call x1, Pallas kernels, lower_inverse(): pl.pallas_call(factor_kernel, out_shape=(shape, shape), in_specs=[pl.Bloc...  165 us
    ppermute x1, waiting for transfers between devices, on_device(): moved = lax.ppermute(mine, ('row', 'col'), moves)  154 us
    all_gather x1, blocking collectives, on_device(): full = lax.all_gather(stacked, ('row', 'col'), axis=1, tiled=True)  68.2 us
    dot_general x1, matrix products, on_device(): update = lax.dot_general(rows_factor, cols_factor, NT, precision=HIGH)  67.4 us
  transfers between devices with their start and end apart: 6, of which 3 were waited for; matrix products, arithmetic and copies ran while one was open for 10% of the time, Pallas kernels for 16%

commit v1 on v0

v1 whole, which is shorter than its diff:
```python
import functools

import jax
import jax.numpy as jnp
from jax import lax
from jax.experimental import pallas as pl
from jax.experimental.pallas import tpu as pltpu
from jax.sharding import PartitionSpec as P

NB = 128
PANELS = 8
CHUNKS = 64
SLACK = 2
AHEAD = 16

HIGHEST = lax.Precision.HIGHEST
HIGH = lax.Precision.HIGH
SIGMA_GAP = 0.5
NT = (((1,), (1,)), ((), ()))
MESH = pl.DeviceIdType.MESH
VMEM = pl.BlockSpec(memory_space=pltpu.VMEM)
ANY = pl.BlockSpec(memory_space=pl.ANY)


def eliminate(block):
    width = block.shape[0]
    rows = lax.broadcasted_iota(jnp.int32, (width, width), 0)
    lanes = lax.broadcasted_iota(jnp.int32, (width, width), 1)

    def step(j, carry):
        left, right = carry
        at_row = rows == j
        row = jnp.sum(jnp.where(at_row, left, 0.0), axis=0, keepdims=True)
        other = jnp.sum(jnp.where(at_row, right, 0.0), axis=0, keepdims=True)
        column = jnp.sum(jnp.where(lanes == j, left, 0.0), axis=1, keepdims=True)
        pivot = jnp.sum(jnp.where(lanes[:1] == j, row, 0.0), axis=1, keepdims=True)
        scale = lax.rsqrt(pivot)
        scale = scale * (1.5 - 0.5 * pivot * scale * scale)
        row = row * scale
        other = other * scale
        column = column * scale
        below = rows > j
        left = jnp.where(below, left - column * row, jnp.where(at_row, row, left))
        right = jnp.where(below, right - column * other, jnp.where(at_row, other, right))
        return (left, right)

    identity = (rows == lanes).astype(jnp.float32)
    upper, inverse = lax.fori_loop(0, width, step, (block, identity))
    upper = jnp.where(lanes >= rows, upper, 0.0)
    return (upper.T, inverse)


def factor_panel(factor_ref, inverse_ref, first):
    order = factor_ref.shape[0]
    last = first + NB
    here = slice(first, last)
    lower, inverse = eliminate(factor_ref[here, here])
    factor_ref[here, here] = lower
    inverse_ref[here, here] = inverse
    if first:
        done = jnp.dot(
            factor_ref[here, :first], inverse_ref[:first, :first], precision=HIGHEST,
            preferred_element_type=jnp.float32,
        )
        inverse_ref[here, :first] = -jnp.dot(
            inverse, done, precision=HIGHEST, preferred_element_type=jnp.float32
        )
    if last < order:
        below = lax.dot_general(
            factor_ref[last:, here], inverse, NT, precision=HIGHEST,
            preferred_element_type=jnp.float32,
        )
        factor_ref[last:, here] = below
        factor_ref[here, last:] = jnp.zeros((NB, order - last), jnp.float32)
        for top in range(last, order, NB):
            factor_ref[top:, top:top + NB] -= lax.dot_general(
                below[top - last:], below[top - last:top - last + NB], NT,
                precision=HIGHEST, preferred_element_type=jnp.float32,
            )


def gather_kernel(row_devices, col_devices, mine_ref, all_ref, send_sem, recv_sem):
    count = row_devices * col_devices
    me = lax.axis_index("row") * col_devices + lax.axis_index("col")
    all_ref[me] = mine_ref[...]

    def copy(k):
        target = lax.rem(me + k, count)
        return pltpu.make_async_remote_copy(
            src_ref=mine_ref, dst_ref=all_ref.at[me], send_sem=send_sem.at[k],
            recv_sem=recv_sem.at[k],
            device_id=(target // col_devices, lax.rem(target, col_devices)),
            device_id_type=MESH,
        )

    def start(k, carry):
        copy(k).start()
        return carry

    def finish(k, carry):
        copy(k).wait_recv()
        copy(k).wait_send()
        return carry

    lax.fori_loop(1, count, start, 0)
    lax.fori_loop(1, count, finish, 0)


def gather_small(mine, row_devices, col_devices):
    count = row_devices * col_devices
    return pl.pallas_call(
        functools.partial(gather_kernel, row_devices, col_devices),
        out_shape=jax.ShapeDtypeStruct((count,) + mine.shape, jnp.float32),
        in_specs=[VMEM],
        out_specs=VMEM,
        scratch_shapes=[pltpu.SemaphoreType.DMA((count,)), pltpu.SemaphoreType.DMA((count,))],
        compiler_params=pltpu.CompilerParams(has_side_effects=True),
        cost_estimate=pl.CostEstimate(flops=10**9, bytes_accessed=10**6, transcendentals=0),
    )(mine)


def sum_kernel(
    row_devices, col_devices, per_col, row_ref, col_ref, all_ref, inbox, mine, send_sem,
    recv_sem, send_back, recv_back,
):
    count = row_devices * col_devices
    row, col = lax.axis_index("row"), lax.axis_index("col")
    me = row * col_devices + col

    def to_row(s):
        return pltpu.make_async_remote_copy(
            src_ref=row_ref.at[s], dst_ref=inbox.at[col], send_sem=send_sem.at[s],
            recv_sem=recv_sem.at[col], device_id=(row, s), device_id_type=MESH,
        )

    def to_col(t):
        target = col * per_col + t
        return target, pltpu.make_async_remote_copy(
            src_ref=col_ref.at[t], dst_ref=inbox.at[col_devices + row],
            send_sem=send_sem.at[col_devices + t], recv_sem=recv_sem.at[col_devices + row],
            device_id=(target // col_devices, lax.rem(target, col_devices)),
            device_id_type=MESH,
        )

    def arrival(slot):
        return pltpu.make_async_remote_copy(
            src_ref=inbox.at[slot], dst_ref=inbox.at[slot], send_sem=send_sem.at[0],
            recv_sem=recv_sem.at[slot], device_id=(row, col), device_id_type=MESH,
        )

    inbox[col] = row_ref[col]
    for s in range(col_devices):
        @pl.when(s != col)
        def _():
            to_row(s).start()
    for t in range(per_col):
        target, copy = to_col(t)

        @pl.when(target != me)
        def _():
            copy.start()

        @pl.when(target == me)
        def _():
            inbox[col_devices + row] = col_ref[t]
    source_col = me // per_col
    for s in range(col_devices):
        @pl.when(s != col)
        def _():
            arrival(s).wait_recv()
    for q in range(row_devices):
        @pl.when(q * col_devices + source_col != me)
        def _():
            arrival(col_devices + q).wait_recv()
    total = inbox[0]
    for slot in range(1, col_devices + row_devices):
        total = total + inbox[slot]
    mine[...] = total
    all_ref[me] = total

    def back(k):
        target = lax.rem(me + k, count)
        return pltpu.make_async_remote_copy(
            src_ref=mine, dst_ref=all_ref.at[me], send_sem=send_back.at[k],
            recv_sem=recv_back.at[k],
            device_id=(target // col_devices, lax.rem(target, col_devices)),
            device_id_type=MESH,
        )

    def start(k, carry):
        back(k).start()
        return carry

    def finish(k, carry):
        back(k).wait_recv()
        back(k).wait_send()
        return carry

    lax.fori_loop(1, count, start, 0)
    lax.fori_loop(1, count, finish, 0)
    for s in range(col_devices):
        @pl.when(s != col)
        def _():
            to_row(s).wait_send()
    for t in range(per_col):
        target, copy = to_col(t)

        @pl.when(target != me)
        def _():
            copy.wait_send()


def sum_parts(row_part, col_part, row_devices, col_devices):
    count = row_devices * col_devices
    piece = row_part.shape[0] // col_devices
    per_col = col_part.shape[0] // piece
    dma = pltpu.SemaphoreType.DMA
    return pl.pallas_call(
        functools.partial(sum_kernel, row_devices, col_devices, per_col),
        out_shape=jax.ShapeDtypeStruct((count, 1, piece), jnp.float32),
        in_specs=[VMEM, VMEM],
        out_specs=VMEM,
        scratch_shapes=[
            pltpu.VMEM((col_devices + row_devices, 1, piece), jnp.float32),
            pltpu.VMEM((1, piece), jnp.float32),
            dma((col_devices + per_col,)),
            dma((col_devices + row_devices,)),
            dma((count,)),
            dma((count,)),
        ],
        compiler_params=pltpu.CompilerParams(has_side_effects=True),
        cost_estimate=pl.CostEstimate(flops=10**9, bytes_accessed=10**6, transcendentals=0),
    )(row_part.reshape(col_devices, 1, piece), col_part.reshape(per_col, 1, piece)).reshape(-1)


def spread_kernel(
    row_devices, col_devices, width, cov_ref, diag_ref, rows_out, cols_out, factor_out,
    inverse_out, rows, cols, factor, inverse, local_sem, row_send, row_recv, col_send,
    col_recv, head_send, head_recv, down_send, down_recv,
):
    tile_rows, lead = rows.shape
    depth = col_devices // width
    half = tile_rows // 2
    step_rows = half // CHUNKS
    part = NB // 2
    row, col = lax.axis_index("row"), lax.axis_index("col")
    z, x = col // width, lax.rem(col, width)
    owner = col // 2
    side = lax.rem(col, 2)
    is_source = col == 0
    is_root = is_source & (row == 0)

    links = (
        (
            ((z == 0) & (x + 1 < width), col + 1),
            ((x >= 1) & (z + 1 < depth), col + width),
            ((z >= 1) & (x == 1), col - 1),
        ),
        (
            ((x == 0) & (z + 1 < depth), col + width),
            ((z >= 1) & (x + 1 < width), col + 1),
            ((z == 1) & (x >= 1), col - width),
        ),
    )
    hops = (
        jnp.where(x >= 1, x + z, jnp.where(z >= 1, z + 2, 0)),
        jnp.where(z >= 1, x + z, jnp.where(x >= 1, x + 2, 0)),
    )
    chain_hops = jnp.where(side == 0, hops[0], hops[1])

    def row_slice(tree, i):
        return pl.ds(pl.multiple_of(tree * half + i * step_rows, step_rows), step_rows)

    def row_copy(tree, link, i, source):
        here = row_slice(tree, i)
        origin = cov_ref.at[here, pl.ds(0, lead)] if source else rows.at[here]
        return pltpu.make_async_remote_copy(
            src_ref=origin, dst_ref=rows.at[here], send_sem=row_send.at[tree, link],
            recv_sem=row_recv.at[tree, i], device_id=(row, links[tree][link][1]),
            device_id_type=MESH,
        )

    def col_copy(i, origin):
        there = pl.ds(pl.multiple_of(i * step_rows, step_rows), step_rows)
        return pltpu.make_async_remote_copy(
            src_ref=origin, dst_ref=cols.at[there], send_sem=col_send.at[0],
            recv_sem=col_recv.at[i], device_id=(row + 1, col), device_id_type=MESH,
        )

    def send_rows(tree, i, source):
        for link in range(3):
            @pl.when(links[tree][link][0])
            def _():
                row_copy(tree, link, i, source).start()

        @pl.when((row == owner) & (side == tree) & (row + 1 < row_devices))
        def _():
            here = row_slice(tree, i)
            origin = cov_ref.at[here, pl.ds(0, lead)] if source else rows.at[here]
            col_copy(i, origin).start()

    def head_slice(tree, p):
        return pl.ds(pl.multiple_of(p * NB + tree * part, part), part)

    def head_copy(tree, link, p):
        here = head_slice(tree, p)
        return pltpu.make_async_remote_copy(
            src_ref=inverse.at[here], dst_ref=inverse.at[here],
            send_sem=head_send.at[tree, link], recv_sem=head_recv.at[tree, p],
            device_id=(row, links[tree][link][1]), device_id_type=MESH,
        )

    def down_copy(p):
        here = pl.ds(pl.multiple_of(p * NB, NB), NB)
        return pltpu.make_async_remote_copy(
            src_ref=inverse.at[here], dst_ref=inverse.at[here], send_sem=down_send.at[0],
            recv_sem=down_recv.at[p], device_id=(row + 1, col), device_id_type=MESH,
        )

    def send_tree(tree, p):
        for link in range(3):
            @pl.when((row == 0) & links[tree][link][0])
            def _():
                head_copy(tree, link, p).start()

    def send_down(p):
        @pl.when(row + 1 < row_devices)
        def _():
            down_copy(p).start()

    own_rows = pltpu.make_async_copy(cov_ref.at[:, pl.ds(0, lead)], rows, local_sem.at[0])
    own_head = pltpu.make_async_copy(
        cov_ref.at[pl.ds(0, lead), pl.ds(0, lead)], factor, local_sem.at[1]
    )

    @pl.when(is_root)
    def _():
        own_head.start()

    @pl.when(is_source)
    def _():
        def first(i, carry):
            send_rows(0, i, True)
            send_rows(1, i, True)
            return carry

        lax.fori_loop(0, AHEAD, first, 0)
        own_rows.start()

    pace = CHUNKS // PANELS

    @pl.when(is_root)
    def _():
        own_head.wait()
        inverse[...] = jnp.zeros_like(inverse)
        below = lax.broadcasted_iota(jnp.int32, (NB, NB), 0)
        across = lax.broadcasted_iota(jnp.int32, (NB, NB), 1)
        for first in range(0, lead, NB):
            here = slice(first, first + NB)
            block = factor[here, here]
            block = jnp.where(below >= across, block, block.T)
            factor[here, here] = block + jnp.where(below == across, diag_ref[:, here], 0.0)
        for p in range(PANELS):
            def more(i, carry):
                send_rows(0, i, True)
                send_rows(1, i, True)
                return carry

            lax.fori_loop(
                min(CHUNKS, AHEAD + pace * p), min(CHUNKS, AHEAD + pace * (p + 1)), more, 0
            )
            factor_panel(factor, inverse, p * NB)
            send_tree(0, p)
            send_tree(1, p)
            send_down(p)

    @pl.when(jnp.logical_not(is_root))
    def _():
        lag = jnp.maximum(hops[0], hops[1]) + row
        head_start = pace + 4

        def step(t, carry):
            @pl.when(is_source & (t + AHEAD < CHUNKS))
            def _():
                send_rows(0, t + AHEAD, True)
                send_rows(1, t + AHEAD, True)

            for tree in range(2):
                i = t - SLACK * hops[tree]

                @pl.when(jnp.logical_not(is_source) & (i >= 0) & (i < CHUNKS))
                def _():
                    row_copy(tree, 0, i, False).wait_recv()
                    send_rows(tree, i, False)

            j = t - SLACK * (chain_hops + row - owner)

            @pl.when((row > owner) & (j >= 0) & (j < CHUNKS))
            def _():
                there = pl.ds(pl.multiple_of(j * step_rows, step_rows), step_rows)
                copy = col_copy(j, cols.at[there])
                copy.wait_recv()

                @pl.when(row + 1 < row_devices)
                def _():
                    copy.start()

            for tree in range(2):
                since = t - head_start - SLACK * hops[tree]
                p = since // pace

                @pl.when((row == 0) & (since >= 0) & (lax.rem(since, pace) == 0) & (p < PANELS))
                def _():
                    head_copy(tree, 0, p).wait_recv()
                    send_tree(tree, p)

            since = t - head_start - SLACK * lag
            p = since // pace

            @pl.when((since >= 0) & (lax.rem(since, pace) == 0) & (p < PANELS))
            def _():
                @pl.when(row > 0)
                def _():
                    down_copy(p).wait_recv()

                send_down(p)

            return carry

        longest = SLACK * (width + depth + 1 + row_devices)
        lax.fori_loop(0, CHUNKS + pace + 8 + longest, step, 0)

    @pl.when(is_source)
    def _():
        own_rows.wait()

    outputs = [
        pltpu.make_async_copy(rows, rows_out, local_sem.at[2]),
        pltpu.make_async_copy(inverse, inverse_out, local_sem.at[3]),
    ]
    for copy in outputs:
        copy.start()

    @pl.when(row > owner)
    def _():
        pltpu.make_async_copy(cols, cols_out, local_sem.at[4]).start()

    @pl.when(row == owner)
    def _():
        here = pl.ds(pl.multiple_of(side * half, half), half)
        pltpu.make_async_copy(rows.at[here], cols_out, local_sem.at[4]).start()

    @pl.when(is_root)
    def _():
        copy = pltpu.make_async_copy(factor, factor_out, local_sem.at[5])
        copy.start()
        copy.wait()

    for copy in outputs:
        copy.wait()

    @pl.when(row >= owner)
    def _():
        pltpu.make_async_copy(cols, cols_out, local_sem.at[4]).wait()

    for tree in range(2):
        for link in range(3):
            @pl.when(links[tree][link][0])
            def _():
                block = rows.at[pl.ds(0, half)]
                pltpu.make_async_remote_copy(
                    src_ref=block, dst_ref=block, send_sem=row_send.at[tree, link],
                    recv_sem=row_recv.at[tree, 0], device_id=(row, links[tree][link][1]),
                    device_id_type=MESH,
                ).wait_send()

            @pl.when((row == 0) & links[tree][link][0])
            def _():
                block = inverse.at[pl.ds(0, lead // 2)]
                pltpu.make_async_remote_copy(
                    src_ref=block, dst_ref=block, send_sem=head_send.at[tree, link],
                    recv_sem=head_recv.at[tree, 0], device_id=(row, links[tree][link][1]),
                    device_id_type=MESH,
                ).wait_send()

    @pl.when((row >= owner) & (row + 1 < row_devices))
    def _():
        pltpu.make_async_remote_copy(
            src_ref=cols, dst_ref=cols, send_sem=col_send.at[0], recv_sem=col_recv.at[0],
            device_id=(row + 1, col), device_id_type=MESH,
        ).wait_send()

    @pl.when(row + 1 < row_devices)
    def _():
        pltpu.make_async_remote_copy(
            src_ref=inverse, dst_ref=inverse, send_sem=down_send.at[0],
            recv_sem=down_recv.at[0], device_id=(row + 1, col), device_id_type=MESH,
        ).wait_send()


def spread(covariance, lead_diag, row_devices, col_devices):
    tile_rows, tile_cols = covariance.shape
    assert tile_rows == 2 * tile_cols
    lead = lead_diag.shape[0]
    width = max(1, row_devices // 2)
    dma = pltpu.SemaphoreType.DMA
    f32 = jnp.float32
    return pl.pallas_call(
        functools.partial(spread_kernel, row_devices, col_devices, width),
        out_shape=(
            jax.ShapeDtypeStruct((tile_rows, lead), f32),
            jax.ShapeDtypeStruct((tile_cols, lead), f32),
            jax.ShapeDtypeStruct((lead, lead), f32),
            jax.ShapeDtypeStruct((lead, lead), f32),
        ),
        in_specs=[ANY, VMEM],
        out_specs=(ANY,) * 4,
        scratch_shapes=[
            pltpu.VMEM((tile_rows, lead), f32),
            pltpu.VMEM((tile_cols, lead), f32),
            pltpu.VMEM((lead, lead), f32),
            pltpu.VMEM((lead, lead), f32),
            dma((6,)),
            dma((2, 3)),
            dma((2, CHUNKS)),
            dma((1,)),
            dma((CHUNKS,)),
            dma((2, 3)),
            dma((2, PANELS)),
            dma((1,)),
            dma((PANELS,)),
        ],
        compiler_params=pltpu.CompilerParams(
            has_side_effects=True, vmem_limit_bytes=50 * 1024 * 1024
        ),
        cost_estimate=pl.CostEstimate(flops=10**11, bytes_accessed=10**8, transcendentals=0),
    )(covariance, lead_diag.reshape(1, lead))


def on_device(covariance, weights, dual_slacks, returns, targets, sector_duals, lengths):
    tile_rows, tile_cols = covariance.shape
    row_devices, col_devices = lax.axis_size("row"), lax.axis_size("col")
    order_total = tile_rows * row_devices
    row_id = lax.axis_index("row")
    col_id = lax.axis_index("col")
    row_start = row_id * tile_rows
    col_start = col_id * tile_cols
    sectors_here = targets.shape[0]
    lead = PANELS * NB

    stacked = jnp.stack([weights, dual_slacks, returns])
    gathered = gather_small(stacked, row_devices, col_devices)
    full = gathered.transpose(1, 0, 2).reshape(3, order_total)
    full_weights, full_slacks, full_returns = full[0], full[1], full[2]
    full_diag = full_slacks / full_weights

    global_rows = row_start + jnp.arange(tile_rows, dtype=jnp.int32)
    global_cols = col_start + jnp.arange(tile_cols, dtype=jnp.int32)
    lower_mask = global_rows[:, None] >= global_cols[None, :]
    strict_mask = global_rows[:, None] > global_cols[None, :]
    weight_rows = lax.dynamic_slice_in_dim(full_weights, row_start, tile_rows)
    weight_cols = lax.dynamic_slice_in_dim(full_weights, col_start, tile_cols)
    row_part = jnp.sum(jnp.where(lower_mask, covariance * weight_cols[None, :], 0.0), axis=1)
    col_part = jnp.sum(jnp.where(strict_mask, covariance * weight_rows[:, None], 0.0), axis=0)
    product = sum_parts(row_part, col_part, row_devices, col_devices)

    rows_raw, cols_raw, factor, inverse = spread(
        covariance, full_diag[:lead], row_devices, col_devices
    )

    sector_ends = jnp.cumsum(lengths)
    offsets = sector_ends - lengths
    mean_gap = jnp.sum(full_weights * full_slacks) / order_total
    sector_first = col_id * sectors_here
    local_offsets = lax.dynamic_slice_in_dim(offsets, sector_first, sectors_here)
    local_ends = lax.dynamic_slice_in_dim(sector_ends, sector_first, sectors_here)
    sector_sizes = lax.dynamic_slice_in_dim(lengths, sector_first, sectors_here).astype(jnp.float32)
    all_assets = jnp.arange(order_total, dtype=jnp.int32)
    column_member = (all_assets[None, :] >= local_offsets[:, None]) & (
        all_assets[None, :] < local_ends[:, None]
    )
    held = jnp.sum(jnp.where(column_member, full_weights[None, :], 0.0), axis=1)
    sector_resid = targets - held / sector_sizes

    def right_sides(start, size):
        index = start + jnp.arange(size, dtype=jnp.int32)
        cut = lambda value: lax.dynamic_slice_in_dim(value, start, size)
        member = (index[:, None] >= offsets[None, :]) & (index[:, None] < sector_ends[None, :])
        prices = jnp.sum(jnp.where(member, sector_duals[None, :], 0.0), axis=1)
        rhs = cut(full_returns) - cut(product) - prices + SIGMA_GAP * mean_gap / cut(full_weights)
        local = (index[:, None] >= local_offsets[None, :]) & (index[:, None] < local_ends[None, :])
        columns = local.astype(jnp.float32) * lax.rsqrt(sector_sizes)[None, :]
        return jnp.concatenate([rhs[:, None], columns], axis=1)

    head_sides = right_sides(0, lead)
    extras = right_sides(row_start, tile_rows)

    solved_head = jnp.dot(inverse, head_sides, precision=HIGHEST)
    back_head = lax.dot_general(inverse, solved_head, (((0,), (0,)), ((), ())), precision=HIGHEST)
    cols_factor = lax.dot_general(cols_raw, inverse, NT, precision=HIGH)
    other = jnp.dot(cols_factor, inverse, precision=HIGH)
    lead_col = (global_cols < lead)[:, None]
    other = jnp.where(lead_col, -jnp.pad(inverse, ((0, tile_cols - lead), (0, 0))), other)

    update = lax.dot_general(rows_raw, other, NT, precision=HIGH)
    diag_rows = lax.dynamic_slice_in_dim(full_diag, row_start, tile_rows)
    on_diagonal = global_rows[:, None] == global_cols[None, :]
    base = jnp.where((global_cols < lead)[None, :], 0.0, covariance)
    base = base + jnp.where(
        on_diagonal & (global_cols >= lead)[None, :], diag_rows[:, None], 0.0
    )
    work = base - update
    lead_part = jnp.pad(factor, ((0, tile_rows - lead), (0, tile_cols - lead)))
    in_head = (global_rows < lead)[:, None] & (global_cols < lead)[None, :]
    work = jnp.where(in_head, lead_part, work)
    factored = jnp.where(lower_mask, work, 0.0)

    extras = extras - jnp.dot(rows_raw, back_head, precision=HIGH)
    top = jnp.where(row_id == 0, solved_head, extras[:lead])
    extras = lax.dynamic_update_slice_in_dim(extras, top, 0, 0)
    return (factored, extras[:, 0], extras[:, 1:], sector_resid)


def solution(mesh):
    return jax.shard_map(
        on_device,
        mesh=mesh,
        in_specs=(
            P("row", "col"),
            P(("row", "col")),
            P(("row", "col")),
            P(("row", "col")),
            P("col"),
            P(),
            P(),
        ),
        out_specs=(P("row", "col"), P("row"), P("row", "col"), P("col")),
        check_vma=False,
    )
```

time: 1030 us -> 500 us (0.49); the launches traced: 1010 us -> 495 us
  waiting for transfers between devices: 568 us -> 0 us
  Pallas kernels: 165 us -> 338 us
  blocking collectives: 68.2 us -> 0 us
  local copies, waits for them, and re-layouts: 32.5 us -> 4.49 us
  other arithmetic: 50.8 us -> 32.4 us
  matrix products: 101 us -> 118 us
  between operations: 17 us -> 1.74 us
    psum x2 -> x0, waiting for transfers between devices: 413 us -> none  [the longest x1 240 us: on_device(): product = lax.psum(partial_value, ('row', 'col'))]
    pallas_call x1 -> x3, Pallas kernels: 165 us -> 338 us  [the longest x1 307 us: spread(): pl.pallas_call(functools.partial(spread_kernel, row_devices, col_devices,...]
    ppermute x1 -> x0, waiting for transfers between devices: 154 us -> none  [on_device(): moved = lax.ppermute(mine, ('row', 'col'), moves)]
    all_gather x1 -> x0, blocking collectives: 68.2 us -> none  [on_device(): full = lax.all_gather(stacked, ('row', 'col'), axis=1, tiled=True)]
    dot_general x4 -> x6, matrix products: 101 us -> 118 us  [the longest x1 64.5 us: on_device(): update = lax.dot_general(rows_raw, other, NT, precision=HIGH)]
    select_n x2 -> x0, other arithmetic: 15.3 us -> none  [the longest x1 12.5 us: on_device(): lead_raw = jnp.where(col_id == 0, covariance[:, :lead], 0.0)]
    add x4 -> x0, other arithmetic: 12.2 us -> none  [the longest x2 6.07 us: on_device(): symmetric = head + jnp.tril(head_raw, -1).T]
    unnamed x39 -> x6, local copies, waits for them, and re-layouts: 10.7 us -> 0.01 us
  transfers between devices with their start and end apart: 6 -> 0, of which waited for: 3 -> 0; matrix products, arithmetic and copies ran while one was open for 10% -> 0% of each run, Pallas kernels for 16% -> 0%
where the time goes in v1:
time: 500 us; the launch traced here: 495 us
  Pallas kernels  338 us (68%)
  matrix products  118 us (24%)
  other arithmetic  32.4 us (6%)
    pallas_call x1, Pallas kernels, spread(): pl.pallas_call(functools.partial(spread_kernel, row_devices, col_devices,...  307 us
    dot_general x1, matrix products, on_device(): update = lax.dot_general(rows_raw, other, NT, precision=HIGH)  64.5 us
    reduce_sum x1, other arithmetic, on_device(): jnp.sum(jnp.where(strict_mask, covariance * weight_rows[:, None], 0.0), a...  16.5 us
    dot_general x1, matrix products, on_device(): cols_factor = lax.dot_general(cols_raw, inverse, NT, precision=HIGH)  15.9 us
    dot_general x1, matrix products, on_device(): other = jnp.dot(cols_factor, inverse, precision=HIGH)  15.7 us
    pallas_call x1, Pallas kernels, gather_small(): pl.pallas_call(functools.partial(gather_kernel, row_devices, col_devices)...  15.6 us
    pallas_call x1, Pallas kernels, sum_parts(): pl.pallas_call(functools.partial(sum_kernel, row_devices, col_devices, pe...  15.3 us
    dot_general x1, matrix products, on_device(): extras = extras - jnp.dot(rows_raw, back_head, precision=HIGH)  11.3 us

profile of v1, /device:TPU:29, one launch (start us, length us, event | category | flops | bytes accessed | tf_op | source)
XLA Modules:
  0.0 495.3 jit_solution(1663334496687258986)
XLA Ops:
  0.6 1.0 reduce-window.9
  1.9 0.8 fusion.18
  2.8 0.9 select_reduce_fusion.3
  3.7 1.3 pad_maximum_fusion.mine_ref
  5.1 2.0 select_reduce_fusion.1
  7.1 15.6 %shard_map.102 = f32[32,3,512]{2,1,0:T(4,128)} custom-call(f32[3,512]{1,0:T(4,128)} %pad_maximum_fusion.mine_ref), custom_call_target="tpu_custom_call" | custom-call | flops 1000000000 | bytes 1000000 | tf_op jit(solution)/shard_map/pallas_call | solution.py:111
  22.7 1.9 fusion.19
  25.3 0.8 fusion.20
  26.1 0.7 select_reduce_fusion.2
  26.8 1.3 divide_subtract_fusion
  28.1 16.5 %select_reduce_fusion = (f32[2048]{0:T(1024)}, f32[4096]{0:T(1024)}) fusion(f32[4096,2048]{1,0:T(8,128)} %cov_ref.1, f32[4096]{0:T(1024)S(1)} %dynamic_slice.41, s32[2048]{0:T(1024)S(1)} %iota_add_fusion.1, s32[4096]{0:T(1024)S(1)} %iota_add_fusion, f32[2048]{0:T(1024)S(1)} %dynamic_slice.40), kind=kLoop, calls=%fused_computation.3 | loop fusion | flops 67102720 | bytes 33628160 | tf_op jit(solution)/shard_map/reduce_sum | solution.py:564
  44.6 15.3 %shard_map.104 = f32[32,1,512]{2,1,0:T(1,128)} custom-call(f32[8,1,512]{2,1,0:T(1,128)} %bitcast.44, f32[4,1,512]{2,1,0:T(1,128)} %bitcast.50), custom_call_target="tpu_custom_call" | custom-call | flops 1000000000 | bytes 1000000 | tf_op jit(solution)/shard_map/pallas_call | solution.py:218
  59.9 0.7 divide_add_fusion
  60.6 0.7 dynamic_slice.48
  61.6 307.4 %shard_map.103 = (f32[4096,1024]{1,0:T(8,128)}, f32[2048,1024]{1,0:T(8,128)}, f32[1024,1024]{1,0:T(8,128)}, f32[1024,1024]{1,0:T(8,128)}) custom-call(f32[4096,2048]{1,0:T(8,128)} %cov_ref.1, f32[1,1024]{1,0:T(1,128)S(1)} %bitcast.33), custom_call_target="tpu_custom_call" | custom-call | flops 99999997952 | bytes 100000000 | tf_op jit(solution)/shard_map/pallas_call | solution.py:508
  368.9 6.2 %fusion.8 = f32[1024,33]{0,1:T(8,128)S(1)} fusion(f32[1024,1024]{1,0:T(8,128)} %get-tuple-element.10, f32[1024,32]{0,1:T(8,128)S(1)} %fusion.13, f32[1024,1]{0,1:T(1,128)S(1)} %subtract_add_fusion), kind=kOutput, calls=%fused_computation.21 | convolution fusion | flops 415269888 | bytes 4464640 | tf_op jit(solution)/shard_map/dot_general | solution.py:598
  375.1 4.8 fusion.23
  380.0 11.3 %convolution_subtract_fusion = f32[4096,33]{0,1:T(8,128)S(1)} fusion(f32[4096,1024]{1,0:T(8,128)} %get-tuple-element.9, f32[1024,33]{0,1:T(8,128)S(1)} %fusion.23, f32[4096,32]{0,1:T(8,128)S(1)} %and_select_fusion, f32[4096,1]{0,1:T(1,128)S(1)} %bitcast.43), kind=kOutput, calls=%fused_computation.7 | convolution fusion | flops 830742528 | bytes 17993728 | tf_op jit(solution)/shard_map/dot_general | solution.py:618
  391.4 15.9 %fusion.21 = f32[2048,1024]{1,0:T(8,128)S(1)} fusion(f32[2048,1024]{1,0:T(8,128)} %get-tuple-element.11, f32[1024,1024]{1,0:T(8,128)S(1)} %copy-done), kind=kOutput, calls=%fused_computation.48 | convolution fusion | flops 12884901888 | bytes 20971520 | tf_op jit(solution)/shard_map/dot_general | solution.py:600
  407.3 15.7 %fusion.22 = f32[2048,1024]{1,0:T(8,128)} fusion(f32[2048,1024]{1,0:T(8,128)S(1)} %fusion.21, f32[1024,1024]{1,0:T(8,128)S(1)} %copy-done), kind=kOutput, calls=%fused_computation.49 | convolution fusion | flops 12884901888 | bytes 20971520 | tf_op jit(solution)/shard_map/dot_general | solution.py:601
  423.0 4.1 fusion.37
  427.1 1.5 slice.50
  428.7 1.9 slice.51
  430.6 64.5 %compare_select_fusion.1 = f32[4096,2048]{1,0:T(8,128)} fusion(f32[4096,2048]{1,0:T(8,128)} %cov_ref.1, f32[1024,1024]{1,0:T(8,128)} %get-tuple-element.8, f32[4096,1024]{1,0:T(8,128)} %get-tuple-element.9, f32[4096]{0:T(1024)S(1)} %dynamic-slice-done, s32[2048]{0:T(1024)S(1)} %iota_add_fusion.1, s32[4096]{0:T(1024)S(1)} %iota_add_fusion, ...), kind=kOutput, calls=%fused_computation.1 | convolution fusion | flops 51623493632 | bytes 96518144 | tf_op jit(solution)/shard_map/dot_general | solution.py:605
  (25 shorter events, 0.7 us)
Async XLA Ops:
  26.1 18.4 %copy-start.2 = (f32[16384]{0:T(1024)}, f32[16384]{0:T(1024)S(1)}, u32[]{:S(2)}) copy-start(f32[16384]{0:T(1024)S(1)} %div.29) | copy-start | bytes 196612
  380.0 11.4 %copy-start = (f32[1024,1024]{1,0:T(8,128)S(1)}, f32[1024,1024]{1,0:T(8,128)}, u32[]{:S(2)}) copy-start(f32[1024,1024]{1,0:T(8,128)} %get-tuple-element.10) | copy-start | bytes 12582916
  391.4 15.9 %copy-start.1 = (f32[4096,33]{0,1:T(8,128)}, f32[4096,33]{0,1:T(8,128)S(1)}, u32[]{:S(2)}) copy-start(f32[4096,33]{0,1:T(8,128)S(1)} %fusion.7) | copy-start | bytes 1622020
  423.0 7.6 %dynamic-slice-start = ((f32[16384]{0:T(1024)}, s32[]{:T(128)}), f32[4096]{0:T(1024)S(1)}, s32[]{:S(2)}) async-start(f32[16384]{0:T(1024)} %copy-done.2, s32[]{:T(128)} %select_n.62), calls=%async_computation | async-start | bytes 33280 | tf_op jit(solution)/shard_map/dynamic_slice | solution.py:606

commit v2 on v1

--- a/solution.py
+++ b/solution.py
@@ -10,8 +10,13 @@
 NB = 128
 PANELS = 8
 CHUNKS = 64
-SLACK = 2
+SLACK = 4
 AHEAD = 16
+PACE = 6
+ROOT_AHEAD = 8
+ROOT_SHARE = 6
+GROUP = 8
+GROUPS = 8
 
 HIGHEST = lax.Precision.HIGHEST
 HIGH = lax.Precision.HIGH
@@ -22,39 +27,51 @@
 ANY = pl.BlockSpec(memory_space=pl.ANY)
 
 
-def eliminate(block):
+def eliminate(block, work):
     width = block.shape[0]
-    rows = lax.broadcasted_iota(jnp.int32, (width, width), 0)
-    lanes = lax.broadcasted_iota(jnp.int32, (width, width), 1)
-
-    def step(j, carry):
-        left, right = carry
-        at_row = rows == j
-        row = jnp.sum(jnp.where(at_row, left, 0.0), axis=0, keepdims=True)
-        other = jnp.sum(jnp.where(at_row, right, 0.0), axis=0, keepdims=True)
-        column = jnp.sum(jnp.where(lanes == j, left, 0.0), axis=1, keepdims=True)
-        pivot = jnp.sum(jnp.where(lanes[:1] == j, row, 0.0), axis=1, keepdims=True)
-        scale = lax.rsqrt(pivot)
-        scale = scale * (1.5 - 0.5 * pivot * scale * scale)
-        row = row * scale
-        other = other * scale
-        column = column * scale
-        below = rows > j
-        left = jnp.where(below, left - column * row, jnp.where(at_row, row, left))
-        right = jnp.where(below, right - column * other, jnp.where(at_row, other, right))
-        return (left, right)
-
-    identity = (rows == lanes).astype(jnp.float32)
-    upper, inverse = lax.fori_loop(0, width, step, (block, identity))
-    upper = jnp.where(lanes >= rows, upper, 0.0)
-    return (upper.T, inverse)
-
-
-def factor_panel(factor_ref, inverse_ref, first):
+    below = lax.broadcasted_iota(jnp.int32, (width, width), 0)
+    across = lax.broadcasted_iota(jnp.int32, (width, width), 1)
+    work[:, :width] = block
+    work[:, width:] = (below == across).astype(jnp.float32)
+    lanes = lax.broadcasted_iota(jnp.int32, (GROUP, width), 1)
+    place = lax.broadcasted_iota(jnp.int32, (GROUP, 1), 0)
+    rows = lax.broadcasted_iota(jnp.int32, (width, 2 * width), 0)
+
+    def step(b, carry):
+        base = pl.multiple_of(b * GROUP, GROUP)
+        piece = work[pl.ds(base, GROUP), :]
+        left = piece[:, :width]
+        small = [
+            jnp.sum(jnp.where(lanes == base + k, left, 0.0), axis=1, keepdims=True)
+            for k in range(GROUP)
+        ]
+        for k in range(GROUP):
+            pivot = small[k][k:k + 1]
+            scale = lax.rsqrt(pivot)
+            scale = scale * (1.5 - 0.5 * pivot * scale * scale)
+            row = piece[k:k + 1] * scale
+            factor = jnp.where(place > k, small[k] * scale, 0.0)
+            piece = jnp.where(place == k, row, piece - factor * row)
+            for other in range(k + 1, GROUP):
+                small[other] = small[other] - factor * (small[other][k:k + 1] * scale)
+        work[pl.ds(base, GROUP), :] = piece
+        change = lax.dot_general(
+            piece[:, :width], piece, (((0,), (0,)), ((), ())), precision=HIGHEST,
+            preferred_element_type=jnp.float32,
+        )
+        work[...] = work[...] - jnp.where(rows >= base + GROUP, change, 0.0)
+        return carry
+
+    lax.fori_loop(0, width // GROUP, step, 0)
+    upper = jnp.where(across >= below, work[:, :width], 0.0)
+    return (upper.T, work[:, width:])
+
+
+def factor_panel(factor_ref, inverse_ref, work_ref, first):
     order = factor_ref.shape[0]
     last = first + NB
     here = slice(first, last)
-    lower, inverse = eliminate(factor_ref[here, here])
+    lower, inverse = eliminate(factor_ref[here, here], work_ref)
     factor_ref[here, here] = lower
     inverse_ref[here, here] = inverse
     if first:
@@ -234,8 +251,8 @@
 
 
 def spread_kernel(
-    row_devices, col_devices, width, cov_ref, diag_ref, rows_out, cols_out, factor_out,
-    inverse_out, rows, cols, factor, inverse, local_sem, row_send, row_recv, col_send,
+    row_devices, col_devices, width, cov_ref, diag_ref, rows_out, other_out, factor_out,
+    inverse_out, both_out, rows, cols, factor, inverse, both, other, stage, work, local_sem, row_send, row_recv, col_send,
     col_recv, head_send, head_recv, down_send, down_recv,
 ):
     tile_rows, lead = rows.shape
@@ -243,6 +260,7 @@
     half = tile_rows // 2
     step_rows = half // CHUNKS
     part = NB // 2
+    group_rows = half // GROUPS
     row, col = lax.axis_index("row"), lax.axis_index("col")
     z, x = col // width, lax.rem(col, width)
     owner = col // 2
@@ -328,6 +346,62 @@
         def _():
             down_copy(p).start()
 
+    def keep_rows(here):
+        pltpu.make_async_copy(rows.at[here], rows_out.at[here], local_sem.at[2]).start()
+
+    def keep_head(p):
+        here = pl.ds(pl.multiple_of(p * NB, NB), NB)
+        pltpu.make_async_copy(inverse.at[here], inverse_out.at[here], local_sem.at[3]).start()
+
+    def keep_own():
+        own_rows.wait()
+        keep_rows(pl.ds(0, tile_rows))
+
+    def add_both(p):
+        here = pl.ds(pl.multiple_of(p * NB, NB), NB)
+
+        def add(k, carry):
+            there = pl.ds(pl.multiple_of(k * NB, NB), NB)
+            both[there, :] += lax.dot_general(
+                inverse[here, there], inverse[here, :], (((0,), (0,)), ((), ())),
+                precision=HIGHEST, preferred_element_type=jnp.float32,
+            )
+            return carry
+
+        lax.fori_loop(0, lead // NB, add, 0)
+
+    def other_group(g):
+        start = pl.multiple_of(g * group_rows, group_rows)
+        there = pl.ds(start, group_rows)
+        direct = is_source & (start < lead)
+
+        @pl.when(direct)
+        def _():
+            other[there, :] = -inverse[there, :]
+
+        @pl.when(jnp.logical_not(direct))
+        def _():
+            @pl.when(row == owner)
+            def _():
+                begin = pl.multiple_of(side * half + g * group_rows, group_rows)
+                stage[...] = rows[pl.ds(begin, group_rows), :]
+
+            @pl.when(row > owner)
+            def _():
+                stage[...] = cols[there, :]
+
+            def part_of(k, carry):
+                lanes = pl.ds(pl.multiple_of(k * 2 * NB, 2 * NB), 2 * NB)
+                other[there, lanes] = jnp.dot(
+                    stage[...], both[:, lanes], precision=HIGHEST,
+                    preferred_element_type=jnp.float32,
+                )
+                return carry
+
+            lax.fori_loop(0, lead // (2 * NB), part_of, 0)
+
+        pltpu.make_async_copy(other.at[there], other_out.at[there], local_sem.at[4]).start()
+
     own_rows = pltpu.make_async_copy(cov_ref.at[:, pl.ds(0, lead)], rows, local_sem.at[0])
     own_head = pltpu.make_async_copy(
         cov_ref.at[pl.ds(0, lead), pl.ds(0, lead)], factor, local_sem.at[1]
@@ -344,14 +418,16 @@
             send_rows(1, i, True)
             return carry
 
-        lax.fori_loop(0, AHEAD, first, 0)
+        lax.fori_loop(0, jnp.where(row == 0, ROOT_AHEAD, AHEAD), first, 0)
         own_rows.start()
 
-    pace = CHUNKS // PANELS
+    pace = PACE
+    both[...] = jnp.zeros_like(both)
 
     @pl.when(is_root)
     def _():
         own_head.wait()
+        keep_own()
         inverse[...] = jnp.zeros_like(inverse)
         below = lax.broadcasted_iota(jnp.int32, (NB, NB), 0)
         across = lax.broadcasted_iota(jnp.int32, (NB, NB), 1)
@@ -360,25 +436,43 @@
             block = factor[here, here]
             block = jnp.where(below >= across, block, block.T)
             factor[here, here] = block + jnp.where(below == across, diag_ref[:, here], 0.0)
+        def more(i, carry):
+            send_rows(0, i, True)
+            send_rows(1, i, True)
+            return carry
+
+        sent = ROOT_AHEAD
         for p in range(PANELS):
-            def more(i, carry):
-                send_rows(0, i, True)
-                send_rows(1, i, True)
-                return carry
-
-            lax.fori_loop(
-                min(CHUNKS, AHEAD + pace * p), min(CHUNKS, AHEAD + pace * (p + 1)), more, 0
-            )
-            factor_panel(factor, inverse, p * NB)
+            factor_panel(factor, inverse, work, p * NB)
             send_tree(0, p)
             send_tree(1, p)
             send_down(p)
+            keep_head(p)
+            following = CHUNKS if p + 1 == PANELS else min(CHUNKS, sent + ROOT_SHARE)
+            lax.fori_loop(sent, following, more, 0)
+            sent = following
+
+        def add_all(p, carry):
+            add_both(p)
+            return carry
+
+        def group_all(g, carry):
+            other_group(g)
+            return carry
+
+        lax.fori_loop(0, PANELS, add_all, 0)
+        lax.fori_loop(0, GROUPS, group_all, 0)
 
     @pl.when(jnp.logical_not(is_root))
     def _():
         lag = jnp.maximum(hops[0], hops[1]) + row
         head_start = pace + 4
 
+        @pl.when(is_source)
+        def _():
+            keep_own()
+
+
         def step(t, carry):
             @pl.when(is_source & (t + AHEAD < CHUNKS))
             def _():
@@ -392,6 +486,7 @@
                 def _():
                     row_copy(tree, 0, i, False).wait_recv()
                     send_rows(tree, i, False)
+                    keep_rows(row_slice(tree, i))
 
             j = t - SLACK * (chain_hops + row - owner)
 
@@ -424,31 +519,24 @@
                     down_copy(p).wait_recv()
 
                 send_down(p)
-
+                keep_head(p)
+                add_both(p)
+
+            def grouped(g, inner):
+                arrived = (g + 1) * (CHUNKS // GROUPS) + SLACK * (chain_hops + row - owner)
+                solved = head_start + SLACK * lag + pace * (PANELS - 1) + g + 1
+
+                @pl.when((row >= owner) & (t == jnp.maximum(arrived, solved)))
+                def _():
+                    other_group(g)
+
+                return inner
+
+            lax.fori_loop(0, GROUPS, grouped, 0)
             return carry
 
         longest = SLACK * (width + depth + 1 + row_devices)
-        lax.fori_loop(0, CHUNKS + pace + 8 + longest, step, 0)
-
-    @pl.when(is_source)
-    def _():
-        own_rows.wait()
-
-    outputs = [
-        pltpu.make_async_copy(rows, rows_out, local_sem.at[2]),
-        pltpu.make_async_copy(inverse, inverse_out, local_sem.at[3]),
-    ]
-    for copy in outputs:
-        copy.start()
-
-    @pl.when(row > owner)
-    def _():
-        pltpu.make_async_copy(cols, cols_out, local_sem.at[4]).start()
-
-    @pl.when(row == owner)
-    def _():
-        here = pl.ds(pl.multiple_of(side * half, half), half)
-        pltpu.make_async_copy(rows.at[here], cols_out, local_sem.at[4]).start()
+        lax.fori_loop(0, max(CHUNKS, pace * PANELS) + pace + 8 + longest, step, 0)
 
     @pl.when(is_root)
     def _():
@@ -456,12 +544,15 @@
         copy.start()
         copy.wait()
 
-    for copy in outputs:
-        copy.wait()
+    pltpu.make_async_copy(rows, rows_out, local_sem.at[2]).wait()
+    pltpu.make_async_copy(inverse, inverse_out, local_sem.at[3]).wait()
+    keep_both = pltpu.make_async_copy(both, both_out, local_sem.at[6])
+    keep_both.start()
+    keep_both.wait()
 
     @pl.when(row >= owner)
     def _():
-        pltpu.make_async_copy(cols, cols_out, local_sem.at[4]).wait()
+        pltpu.make_async_copy(other, other_out, local_sem.at[4]).wait()
 
     for tree in range(2):
         for link in range(3):
@@ -512,15 +603,20 @@
             jax.ShapeDtypeStruct((tile_cols, lead), f32),
             jax.ShapeDtypeStruct((lead, lead), f32),
             jax.ShapeDtypeStruct((lead, lead), f32),
+            jax.ShapeDtypeStruct((lead, lead), f32),
         ),
         in_specs=[ANY, VMEM],
-        out_specs=(ANY,) * 4,
+        out_specs=(ANY,) * 5,
         scratch_shapes=[
             pltpu.VMEM((tile_rows, lead), f32),
             pltpu.VMEM((tile_cols, lead), f32),
             pltpu.VMEM((lead, lead), f32),
             pltpu.VMEM((lead, lead), f32),
-            dma((6,)),
+            pltpu.VMEM((lead, lead), f32),
+            pltpu.VMEM((tile_cols, lead), f32),
+            pltpu.VMEM((tile_cols // GROUPS, lead), f32),
+            pltpu.VMEM((NB, 2 * NB), f32),
+            dma((7,)),
             dma((2, 3)),
             dma((2, CHUNKS)),
             dma((1,)),
@@ -531,7 +627,7 @@
             dma((PANELS,)),
         ],
         compiler_params=pltpu.CompilerParams(
-            has_side_effects=True, vmem_limit_bytes=50 * 1024 * 1024
+            has_side_effects=True, vmem_limit_bytes=58 * 1024 * 1024
         ),
         cost_estimate=pl.CostEstimate(flops=10**11, bytes_accessed=10**8, transcendentals=0),
     )(covariance, lead_diag.reshape(1, lead))
@@ -564,7 +660,7 @@
     col_part = jnp.sum(jnp.where(strict_mask, covariance * weight_rows[:, None], 0.0), axis=0)
     product = sum_parts(row_part, col_part, row_devices, col_devices)
 
-    rows_raw, cols_raw, factor, inverse = spread(
+    rows_raw, other, factor, inverse, both = spread(
         covariance, full_diag[:lead], row_devices, col_devices
     )
 
@@ -595,12 +691,8 @@
     head_sides = right_sides(0, lead)
     extras = right_sides(row_start, tile_rows)
 
-    solved_head = jnp.dot(inverse, head_sides, precision=HIGHEST)
-    back_head = lax.dot_general(inverse, solved_head, (((0,), (0,)), ((), ())), precision=HIGHEST)
-    cols_factor = lax.dot_general(cols_raw, inverse, NT, precision=HIGH)
-    other = jnp.dot(cols_factor, inverse, precision=HIGH)
-    lead_col = (global_cols < lead)[:, None]
-    other = jnp.where(lead_col, -jnp.pad(inverse, ((0, tile_cols - lead), (0, 0))), other)
+    solved_head = jnp.dot(inverse, head_sides, precision=HIGH)
+    back_head = jnp.dot(both, head_sides, precision=HIGH)
 
     update = lax.dot_general(rows_raw, other, NT, precision=HIGH)
     diag_rows = lax.dynamic_slice_in_dim(full_diag, row_start, tile_rows)

time: 500 us -> 453 us (0.906)
  matrix products: 118 us -> 83.9 us
    dot_general x4 -> x2, matrix products: 42.6 us -> 6.12 us  [the longest x1 4.13 us: on_device(): back_head = jnp.dot(both, head_sides, precision=HIGH)]
where the time goes in v2:
time: 453 us; the launch traced here: 452 us
  Pallas kernels  336 us (74%)
  matrix products  83.9 us (19%)
  other arithmetic  28.2 us (6%)
    pallas_call x1, Pallas kernels, spread(): pl.pallas_call(functools.partial(spread_kernel, row_devices, col_devices,...  305 us
    dot_general x1, matrix products, on_device(): update = lax.dot_general(rows_raw, other, NT, precision=HIGH)  66.6 us
    reduce_sum x1, other arithmetic, on_device(): jnp.sum(jnp.where(strict_mask, covariance * weight_rows[:, None], 0.0), a...  16.4 us
    pallas_call x1, Pallas kernels, gather_small(): pl.pallas_call(functools.partial(gather_kernel, row_devices, col_devices)...  15.6 us
    pallas_call x1, Pallas kernels, sum_parts(): pl.pallas_call(functools.partial(sum_kernel, row_devices, col_devices, pe...  15.3 us
    dot_general x1, matrix products, on_device(): extras = extras - jnp.dot(rows_raw, back_head, precision=HIGH)  11.2 us

profile of v2, /device:TPU:29, one launch (start us, length us, event | category | flops | bytes accessed | tf_op | source)
XLA Modules:
  0.0 452.3 jit_solution(11714384299739014324)
XLA Ops:
  0.6 1.0 reduce-window.9
  1.7 0.1 slice_reduce_fusion
  1.9 0.8 fusion.11
  2.8 0.9 select_reduce_fusion.3
  3.7 1.3 pad_maximum_fusion.3.mine_ref
  5.1 2.0 select_reduce_fusion.1
  7.1 15.6 %shard_map.102 = f32[32,3,512]{2,1,0:T(4,128)} custom-call(f32[3,512]{1,0:T(4,128)} %pad_maximum_fusion.3.mine_ref), custom_call_target="tpu_custom_call" | custom-call | flops 1000000000 | bytes 1000000 | tf_op jit(solution)/shard_map/pallas_call | solution.py:128
  22.7 1.9 fusion.12
  25.3 0.8 fusion.13
  26.1 0.7 select_reduce_fusion.2
  26.8 1.3 divide_subtract_fusion
  28.1 0.6 slice.47
  28.7 16.4 %select_reduce_fusion = (f32[2048]{0:T(1024)}, f32[4096]{0:T(1024)}) fusion(f32[4096,2048]{1,0:T(8,128)} %cov_ref.1, f32[4096]{0:T(1024)S(1)} %dynamic_slice.41, s32[2048]{0:T(1024)S(1)} %iota_add_fusion.1, s32[4096]{0:T(1024)S(1)} %iota_add_fusion, f32[2048]{0:T(1024)S(1)} %dynamic_slice.40), kind=kLoop, calls=%fused_computation.3 | loop fusion | flops 67102720 | bytes 33628160 | tf_op jit(solution)/shard_map/reduce_sum | solution.py:660
  45.1 15.3 %shard_map.104 = f32[32,1,512]{2,1,0:T(1,128)} custom-call(f32[8,1,512]{2,1,0:T(1,128)} %bitcast.37, f32[4,1,512]{2,1,0:T(1,128)} %bitcast.43), custom_call_target="tpu_custom_call" | custom-call | flops 1000000000 | bytes 1000000 | tf_op jit(solution)/shard_map/pallas_call | solution.py:235
  60.4 0.7 divide_add_fusion
  61.2 0.7 dynamic_slice.48
  62.0 0.1 and_select_fusion
  62.1 304.8 %shard_map.103 = (f32[4096,1024]{1,0:T(8,128)}, f32[2048,1024]{1,0:T(8,128)}, f32[1024,1024]{1,0:T(8,128)}, f32[1024,1024]{1,0:T(8,128)}, f32[1024,1024]{1,0:T(8,128)}) custom-call(f32[4096,2048]{1,0:T(8,128)} %cov_ref.1, f32[1,1024]{1,0:T(1,128)} %bitcast.46), custom_call_target="tpu_custom_call" | custom-call | flops 99999997952 | bytes 100000000 | tf_op jit(solution)/shard_map/pallas_call | solution.py:599
  366.9 4.1 fusion.4
  371.1 11.2 %convolution_subtract_fusion = f32[4096,33]{0,1:T(8,128)S(1)} fusion(f32[4096,1024]{1,0:T(8,128)} %get-tuple-element.10, f32[1024,33]{0,1:T(8,128)S(1)} %fusion.4, f32[4096,32]{0,1:T(8,128)S(1)} %and_select_fusion, f32[4096,1]{0,1:T(1,128)S(1)} %bitcast.36), kind=kOutput, calls=%fused_computation.4 | convolution fusion | flops 830742528 | bytes 17993728 | tf_op jit(solution)/shard_map/dot_general | solution.py:710
  382.2 2.0 fusion.2
  384.2 0.6 slice.50
  384.8 0.8 slice.51
  385.7 66.6 %compare_select_fusion.1 = f32[4096,2048]{1,0:T(8,128)} fusion(f32[4096,2048]{1,0:T(8,128)} %cov_ref.1, f32[1024,1024]{1,0:T(8,128)S(1)} %copy-done.2, f32[4096,1024]{1,0:T(8,128)} %get-tuple-element.10, f32[2048,1024]{1,0:T(8,128)} %get-tuple-element.11, f32[4096]{0:T(1024)S(1)} %dynamic-slice-done, s32[2048]{0:T(1024)S(1)} %iota_add_fusion.1, ...), kind=kOutput, calls=%fused_computation.1 | convolution fusion | flops 51623493632 | bytes 96518144 | tf_op jit(solution)/shard_map/dot_general | solution.py:697
  (21 shorter events, 0.4 us)
Async XLA Ops:
  26.1 19.0 %copy-start.1 = (f32[16384]{0:T(1024)}, f32[16384]{0:T(1024)S(1)}, u32[]{:S(2)}) copy-start(f32[16384]{0:T(1024)S(1)} %div.29) | copy-start | bytes 196612
  371.0 11.2 %copy-start = (f32[1024,1024]{1,0:T(8,128)S(1)}, f32[1024,1024]{1,0:T(8,128)}, u32[]{:S(2)}) copy-start(f32[1024,1024]{1,0:T(8,128)} %get-tuple-element.13) | copy-start | bytes 12582916
  371.0 14.6 %dynamic-slice-start = ((f32[16384]{0:T(1024)}, s32[]{:T(128)}), f32[4096]{0:T(1024)S(1)}, s32[]{:S(2)}) async-start(f32[16384]{0:T(1024)} %copy-done.1, s32[]{:T(128)} %select_n.58), calls=%async_computation | async-start | bytes 33280 | tf_op jit(solution)/shard_map/dynamic_slice | solution.py:698
  371.0 14.6 %copy-start.2 = (f32[1024,1024]{1,0:T(8,128)S(1)}, f32[1024,1024]{1,0:T(8,128)}, u32[]{:S(2)}) copy-start(f32[1024,1024]{1,0:T(8,128)} %get-tuple-element.9) | copy-start | bytes 12582916
